TPU v7x, 32 devices: a whole 2x2x4 slice. The times are simulated.
32 devices in a mesh: groups: 2 (over x), tp: 8 (over z, y), role: 2 (over core).
Axes of the slice: x: 2, y: 2, z: 4, core: 2. Of those that a mesh axis runs over, the one named last changes fastest.
Arguments:
- rows_in: bfloat16 [2, 1024, 8192], P('role', 'groups', 'tp'), parts along dimension 1, may hold values from -6 to 6
- norm_gain: bfloat16 [8192], replicated, may hold values from 0.5 to 4
- q_words: int32 [1024, 8192], P(None, 'tp'), may hold values from -2147483648 to 2147483646
- q_scales: bfloat16 [64, 8192], P(None, 'tp'), may hold values from 0.0011978149 to 0.0047912598
- kv_words: int32 [8, 1024, 256], P('tp'), may hold values from -2147483648 to 2147483646, as said below
- kv_scales: bfloat16 [8, 64, 256], P('tp'), may hold values from 0.0012 to 0.0048, as said below
- o_words: int32 [1024, 8192], P('tp'), may hold values from -2147483648 to 2147483646
- o_scales: bfloat16 [64, 8192], P('tp'), may hold values from 0.0011978149 to 0.0047912598
- kv_pool: bfloat16 [8, 2048, 16, 256], P('tp', 'groups'), parts along dimension 1, may hold values from -120 to 120, as said below
- prompt_pages: int32 [32], P('groups'), parts along dimension 0, may hold values from 1 to 8, 32 in all
- page_slots: int32 [64], P('groups'), parts along dimension 0, may hold values from 0 to 1023, as said below
- block_tables: int32 [992, 16], P('groups'), parts along dimension 0, may hold values from 0 to 1023, as said below
- cache_lens: int32 [992], P('groups'), parts along dimension 0, may hold values from 1 to 256
Outputs:
- layer_out: bfloat16 [2, 1024, 8192], P('role', 'groups', 'tp'), parts along dimension 1
There are 2 independent parts, one for each index of `groups`. A program takes and returns all parts, laid end to end along the dimension named above; an argument that names none is the same for every part. Nothing has to cross between parts.
Inputs may be any that keep to these rules, and one draw needn't show every extreme that they name: `kv_words`: entries t and u are equal whenever t * 8 // 8 equals u * 8 // 8. `kv_scales`: entries t and u are equal whenever t * 8 // 8 equals u * 8 // 8. `kv_pool`: entries t and u are equal whenever t * 8 // 8 equals u * 8 // 8. `page_slots`: distinct pages; entry j receives the j-th page of the prompts taken in order. `block_tables`: no entry is one of page_slots; sequences may share pages.
All inputs are finite; a program needn't handle non-finite values.
Results may differ from a plain program's by a relative error of at most 0.015.
The roundings to bfloat16 on the way count: a program that leaves them out, or rounds other values in their place, can miss the bound.
Values may be sent and summed in bfloat16 or wider, within the bound.
A program may use at most 192 MiB of HBM per device.

v0:
```python
import jax
import jax.numpy as jnp
from jax import lax
from jax.sharding import PartitionSpec as P

HD = 128


def passed_along(block, axis, distance):
    devices = range(lax.axis_size(axis))
    route = [(i - distance, i) for i in devices if i - distance in devices]
    return lax.ppermute(block, axis, route)


def unpack_words(words, scales):
    shifts = jnp.arange(8, dtype=jnp.int32) * 4
    nibbles = jnp.bitwise_and(jnp.right_shift(words[:, None, :], shifts[None, :, None]), 15) - 8
    values = nibbles.reshape(words.shape[0] * 8, words.shape[1]).astype(jnp.float32)
    group = values.shape[0] // scales.shape[0]
    spread = jnp.repeat(scales.astype(jnp.float32), group, axis=0)
    return (values * spread).astype(jnp.bfloat16)


def rms_normed(rows, gain):
    wide = rows.astype(jnp.float32)
    inverse = lax.rsqrt(jnp.mean(wide * wide, axis=-1, keepdims=True) + 1e-05)
    return (wide * inverse * gain.astype(jnp.float32)).astype(jnp.bfloat16)


def rotate(heads, positions):
    half = heads.shape[-1] // 2
    freq = 500000.0 ** (-jnp.arange(half, dtype=jnp.float32) * 2.0 / heads.shape[-1])
    angle = positions.astype(jnp.float32)[:, None, None] * freq[None, None, :]
    cosine = jnp.cos(angle)
    sine = jnp.sin(angle)
    first = heads[..., :half]
    second = heads[..., half:]
    return jnp.concatenate(
        [first * cosine - second * sine, second * cosine + first * sine], axis=-1
    )


def layout(prompt_pages, page_slots, block_tables, cache_lens, rows):
    page = rows // page_slots.shape[0]
    count = prompt_pages.shape[0]
    ends = jnp.cumsum(prompt_pages) * page
    starts = ends - prompt_pages * page
    index = jnp.arange(rows, dtype=jnp.int32)
    member = (index[:, None] >= starts[None, :]) & (index[:, None] < ends[None, :])
    doc = jnp.sum(jnp.where(member, jnp.arange(count, dtype=jnp.int32)[None, :], 0), axis=1)
    prefill_pos = index - jnp.sum(jnp.where(member, starts[None, :], 0), axis=1)
    span = block_tables.shape[1]
    picks = jnp.minimum(
        starts[:, None] // page + jnp.arange(span, dtype=jnp.int32)[None, :],
        page_slots.shape[0] - 1,
    )
    prompt_table = page_slots[picks]
    table = jnp.concatenate([prompt_table, block_tables], axis=0)
    lengths = jnp.concatenate([prompt_pages * page, cache_lens])
    return (doc, prefill_pos, table, lengths)


def prefill_attend(query, keys, values, doc):
    rows = query.shape[0]
    block = min(512, rows)
    score_scale = query.shape[-1] ** (-0.5)
    index = jnp.arange(rows, dtype=jnp.int32)

    def prefill_one_block(start):
        logit_scores = (
            jnp.einsum("qhd,kd->hqk", query, keys, preferred_element_type=jnp.float32) * score_scale
        )
        own = start + jnp.arange(block, dtype=jnp.int32)
        allowed = (doc[:, None] == doc[None, :]) & (index[None, :] <= own[:, None])
        logit_scores = jnp.where(allowed[None], logit_scores, -1e30)
        attention_probs = jax.nn.softmax(logit_scores, axis=-1).astype(jnp.bfloat16)
        return jnp.einsum(
            "hqk,kd->qhd", attention_probs, values, preferred_element_type=jnp.float32
        ).astype(jnp.bfloat16)

    starts = jnp.arange(0, rows, block, dtype=jnp.int32)
    done = lax.map(prefill_one_block, starts)
    return done.reshape(rows, query.shape[1], query.shape[2])


def decode_attend(query, key_self, value_self, cache, table, lengths):
    rows = query.shape[0]
    block = min(128, rows)
    score_scale = query.shape[-1] ** (-0.5)
    head_dim = query.shape[-1]

    def decode_one_block(start):
        partial_query = lax.dynamic_slice_in_dim(query, start, block, 0)
        part_table = lax.dynamic_slice_in_dim(table, start, block, 0)
        part_len = lax.dynamic_slice_in_dim(lengths, start, block, 0)
        pages = cache[part_table]
        pages = pages.reshape(block, pages.shape[1] * pages.shape[2], pages.shape[3])
        own_key = lax.dynamic_slice_in_dim(key_self, start, block, 0)
        own_value = lax.dynamic_slice_in_dim(value_self, start, block, 0)
        gathered_keys = jnp.concatenate([pages[..., :head_dim], own_key[:, None, :]], axis=1)
        gathered_values = jnp.concatenate([pages[..., head_dim:], own_value[:, None, :]], axis=1)
        logit_scores = (
            jnp.einsum(
                "jai,jri->jar", partial_query, gathered_keys, preferred_element_type=jnp.float32
            )
            * score_scale
        )
        spots = jnp.arange(pages.shape[1], dtype=jnp.int32)
        valid = jnp.concatenate(
            [spots[None, :] < part_len[:, None], jnp.ones((block, 1), dtype=bool)], axis=1
        )
        logit_scores = jnp.where(valid[:, None, :], logit_scores, -1e30)
        attention_probs = jax.nn.softmax(logit_scores, axis=-1).astype(jnp.bfloat16)
        return jnp.einsum(
            "cwt,ctr->cwr", attention_probs, gathered_values, preferred_element_type=jnp.float32
        ).astype(jnp.bfloat16)

    starts = jnp.arange(0, rows, block, dtype=jnp.int32)
    done = lax.map(decode_one_block, starts)
    return done.reshape(rows, query.shape[1], query.shape[2])


def local(
    rows_in,
    norm_gain,
    q_words,
    q_scales,
    kv_words,
    kv_scales,
    o_words,
    o_scales,
    kv_pool,
    prompt_pages,
    page_slots,
    block_tables,
    cache_lens,
):
    side = lax.axis_index("role")
    whole = lax.all_gather(rows_in[0], "tp", axis=1, tiled=True)
    rows = whole.shape[0]
    normed = rms_normed(whole, norm_gain)
    doc, prefill_pos, table, lengths = layout(
        prompt_pages, page_slots, block_tables, cache_lens, rows
    )
    positions = jnp.where(side == 0, prefill_pos, lengths)
    w_query = unpack_words(q_words, q_scales)
    w_keyval = unpack_words(kv_words[0], kv_scales[0])
    projected = jnp.dot(normed, w_query, preferred_element_type=jnp.float32)
    query = rotate(projected.reshape(rows, -1, HD), positions).astype(jnp.bfloat16)
    keyval = jnp.dot(normed, w_keyval, preferred_element_type=jnp.float32)
    key_new = rotate(keyval[:, None, :HD], positions)[:, 0].astype(jnp.bfloat16)
    value_new = keyval[:, HD:].astype(jnp.bfloat16)
    fresh = jnp.concatenate([key_new, value_new], axis=1)
    arrived = passed_along(fresh, "role", 1)
    pool = kv_pool[0]

    def run_prefill():
        return prefill_attend(query, key_new, value_new, doc)

    def run_decode():
        cache = pool.at[page_slots].set(arrived.reshape(-1, pool.shape[1], pool.shape[2]))
        return decode_attend(query, key_new, value_new, cache, table, lengths)

    attention_output = lax.cond(side == 0, run_prefill, run_decode).reshape(rows, -1)
    column_words, column_scales = (
        lax.all_to_all(o_words, "tp", split_axis=1, concat_axis=0, tiled=True),
        lax.all_to_all(o_scales, "tp", split_axis=1, concat_axis=0, tiled=True),
    )
    w_columns = unpack_words(column_words, column_scales)
    summed = jnp.dot(
        lax.all_gather(attention_output, "tp", axis=1, tiled=True),
        w_columns,
        preferred_element_type=jnp.float32,
    )
    return summed.astype(jnp.bfloat16)[None]


def solution(mesh):
    return jax.shard_map(
        local,
        mesh=mesh,
        in_specs=(
            P("role", "groups", "tp"),
            P(),
            P(None, "tp"),
            P(None, "tp"),
            P("tp", None, None),
            P("tp", None, None),
            P("tp", None),
            P("tp", None),
            P("tp", "groups", None, None),
            P("groups"),
            P("groups"),
            P("groups", None),
            P("groups"),
        ),
        out_specs=P("role", "groups", "tp"),
        check_vma=False,
    )
```

profile of v0, /device:TPU:1, one launch (start us, length us, event | category | flops | bytes accessed | tf_op | source)
XLA Modules:
  0.0 628.8 jit_solution(2411053265637678212)
XLA Ops:
  6.5 7.1 %copy.117 = bf16[1,1024,16,256]{3,2,1,0:T(8,128)(2,1)} copy(bf16[1,1024,16,256]{3,2,1,0:T(8,128)(2,1)} %param.25) | data formatting | bytes 16777216
  13.7 6.4 %all-to-all-start.1 = ((bf16[8,8,1024]{2,0,1:T(8,128)(2,1)}), bf16[8,8,1024]{2,0,1:T(8,128)(2,1)S(1)}, u32[]{:S(2)}, u32[]{:S(2)}) async-start(bf16[8,8,1024]{2,0,1:T(8,128)(2,1)} %bitcast.31), calls=%async_computation.1 | async-start | bytes 262144 | tf_op jit(solution)/shard_map/all_to_all | solution.py:167
  20.1 5.7 copy.76
  38.6 169.3 %all-to-all-done = s32[128,8,1024]{0,2,1:T(8,128)} async-done(((s32[128,8,1024]{0,2,1:T(8,128)}), s32[128,8,1024]{0,2,1:T(8,128)}, u32[]{:S(2)}, u32[]{:S(2)}) %all-to-all-start) | async-done | bytes 4194336 | tf_op jit(solution)/shard_map/all_to_all | solution.py:166
  207.9 5.4 copy.77
  213.3 17.7 %fusion.43 = (bf16[8192,1024]{1,0:T(8,128)(2,1)}, bf16[8192,1024]{1,0:T(8,128)(2,1)}) fusion(f32[64,1024]{1,0:T(8,128)S(1)} %convert_bitcast_fusion, s32[1024,1024]{1,0:T(8,128)} %bitcast.137, s32[8192]{0:T(1024)S(1)} %shift_right_arithmetic.68, f32[64,1024]{1,0:T(8,128)S(1)} %convert_element_type.93, s32[1024,1024]{1,0:T(8,128)} %param.19), kind=kLoop, calls=%fused_computation.53 | loop fusion | flops 100663296 | bytes 42500096 | tf_op jit(solution)/shard_map/convert_element_type | solution.py:21
  231.0 21.3 %copy.84 = bf16[1024,8192]{1,0:T(8,128)(2,1)} copy(bf16[1024,8192]{0,1:T(8,128)(2,1)} %bitcast.136) | data formatting | bytes 33554432 | tf_op jit(solution)/shard_map/dot_general | solution.py:148
  265.2 12.3 %fusion.54 = f32[512,8,128]{0,2,1:T(8,128)S(1)} fusion(bf16[8,128,8192]{2,1,0:T(8,128)(2,1)} %bitcast.138, bf16[1,512,8192]{2,1,0:T(8,128)(2,1)S(1)} %copy-done.1, f32[8192]{0:T(1024)S(1)} %convert_element_type.84, f32[512]{0:T(512)S(1)} %add_rsqrt_fusion), kind=kOutput, calls=%fused_computation.69 | convolution fusion | flops 8606711808 | bytes 27297792 | tf_op jit(solution)/shard_map/dot_general | solution.py:148
  278.0 205.5 %conditional.1 = (bf16[512,8,128]{2,0,1:T(8,128)(2,1)S(1)}) conditional(s32[]{:T(128)} %convert_element_type.82, (bf16[1,1024,16,256]{3,2,1,0:T(8,128)(2,1)}, s32[32]{0:T(128)S(1)}, bf16[512,256]{0,1:T(8,128)(2,1)S(1)}, s32[512]{0:T(512)S(1)}, bf16[512,8,128]{0,2,1:T(8,128)(2,1)S(1)}, /*index=5*/s32[512,16]{0,1:T(8,128)S(1)}, ...), branch_computations={%region_3.9_spmd, %region_9.13_spmd} | conditional | flops 1087651840 | bytes 90089912 | solution.py:164
  282.0 201.2 %while.9 = (s32[]{:T(128)}, bf16[4,128,8,128]{3,1,0,2:T(8,128)(2,1)S(1)}, s32[4]{0:T(128)S(1)}, s32[512]{0:T(512)S(1)}, bf16[512,8,128]{0,2,1:T(8,128)(2,1)S(1)}...) while((s32[]{:T(128)}, ...), condition=%wide.region_8.8_spmd, body=%wide.region_5.7_spmd.sunk | while | flops 170178816 | bytes 88778672 | solution.py:119
  285.0 22.2 %gather_fusion = bf16[2048,16,256]{2,1,0:T(8,128)(2,1)} fusion(bf16[1024,16,256]{2,1,0:T(8,128)(2,1)} %get-tuple-element.313, s32[2048]{0:T(1024)S(1)} %broadcast_clamp_fusion.2), kind=kCustom, calls=%fused_computation.clone.1 | custom fusion | bytes 33562624 | tf_op jit(solution)/shard_map/cond/branch_0_fun/while/body/eval_jaxpr/gather | solution.py:96
  307.2 11.7 %fusion.100 = (bf16[128,256,128]{2,1,0:T(8,128)(2,1)}, bf16[128,256,128]{2,1,0:T(8,128)(2,1)}) fusion(bf16[128,256,256]{2,1,0:T(8,128)(2,1)} %bitcast.134), kind=kLoop, calls=%fused_computation.121.clone.1 | loop fusion | bytes 33554432 | tf_op jit(solution)/shard_map/cond/branch_0_fun/while/body/eval_jaxpr/slice | solution.py:100
  319.7 7.1 %fusion.101 = (f32[128,8]{1,0:T(8,128)S(1)}, f32[128,8,257]{2,1,0:T(8,128)}) fusion(bf16[128,8,128]{2,1,0:T(8,128)(2,1)S(1)} %copy.103, bf16[128,1,128]{2,1,0:T(2,128)(2,1)S(1)} %copy.105, bf16[128,256,128]{2,1,0:T(8,128)(2,1)} %get-tuple-element.278, pred[128,257]{1,0:T(8,128)(4,1)S(1)} %concatenate.36), kind=kOutput, calls=%fused_computation.122.clone.1 | convolution fusion | flops 85266688 | bytes 9773184 | tf_op jit(solution)/shard_map/cond/branch_0_fun/while/body/eval_jaxpr/sub | solution.py:113
  335.3 22.2 %gather_fusion = bf16[2048,16,256]{2,1,0:T(8,128)(2,1)} fusion(bf16[1024,16,256]{2,1,0:T(8,128)(2,1)} %get-tuple-element.313, s32[2048]{0:T(1024)S(1)} %broadcast_clamp_fusion.2), kind=kCustom, calls=%fused_computation.clone.1 | custom fusion | bytes 33562624 | tf_op jit(solution)/shard_map/cond/branch_0_fun/while/body/eval_jaxpr/gather | solution.py:96
  357.5 11.7 %fusion.100 = (bf16[128,256,128]{2,1,0:T(8,128)(2,1)}, bf16[128,256,128]{2,1,0:T(8,128)(2,1)}) fusion(bf16[128,256,256]{2,1,0:T(8,128)(2,1)} %bitcast.134), kind=kLoop, calls=%fused_computation.121.clone.1 | loop fusion | bytes 33554432 | tf_op jit(solution)/shard_map/cond/branch_0_fun/while/body/eval_jaxpr/slice | solution.py:100
  370.0 7.1 %fusion.101 = (f32[128,8]{1,0:T(8,128)S(1)}, f32[128,8,257]{2,1,0:T(8,128)}) fusion(bf16[128,8,128]{2,1,0:T(8,128)(2,1)S(1)} %copy.103, bf16[128,1,128]{2,1,0:T(2,128)(2,1)S(1)} %copy.105, bf16[128,256,128]{2,1,0:T(8,128)(2,1)} %get-tuple-element.278, pred[128,257]{1,0:T(8,128)(4,1)S(1)} %concatenate.36), kind=kOutput, calls=%fused_computation.122.clone.1 | convolution fusion | flops 85266688 | bytes 9773184 | tf_op jit(solution)/shard_map/cond/branch_0_fun/while/body/eval_jaxpr/sub | solution.py:113
  385.6 22.2 %gather_fusion = bf16[2048,16,256]{2,1,0:T(8,128)(2,1)} fusion(bf16[1024,16,256]{2,1,0:T(8,128)(2,1)} %get-tuple-element.313, s32[2048]{0:T(1024)S(1)} %broadcast_clamp_fusion.2), kind=kCustom, calls=%fused_computation.clone.1 | custom fusion | bytes 33562624 | tf_op jit(solution)/shard_map/cond/branch_0_fun/while/body/eval_jaxpr/gather | solution.py:96
  407.8 11.7 %fusion.100 = (bf16[128,256,128]{2,1,0:T(8,128)(2,1)}, bf16[128,256,128]{2,1,0:T(8,128)(2,1)}) fusion(bf16[128,256,256]{2,1,0:T(8,128)(2,1)} %bitcast.134), kind=kLoop, calls=%fused_computation.121.clone.1 | loop fusion | bytes 33554432 | tf_op jit(solution)/shard_map/cond/branch_0_fun/while/body/eval_jaxpr/slice | solution.py:100
  420.3 7.1 %fusion.101 = (f32[128,8]{1,0:T(8,128)S(1)}, f32[128,8,257]{2,1,0:T(8,128)}) fusion(bf16[128,8,128]{2,1,0:T(8,128)(2,1)S(1)} %copy.103, bf16[128,1,128]{2,1,0:T(2,128)(2,1)S(1)} %copy.105, bf16[128,256,128]{2,1,0:T(8,128)(2,1)} %get-tuple-element.278, pred[128,257]{1,0:T(8,128)(4,1)S(1)} %concatenate.36), kind=kOutput, calls=%fused_computation.122.clone.1 | convolution fusion | flops 85266688 | bytes 9773184 | tf_op jit(solution)/shard_map/cond/branch_0_fun/while/body/eval_jaxpr/sub | solution.py:113
  435.9 22.2 %gather_fusion = bf16[2048,16,256]{2,1,0:T(8,128)(2,1)} fusion(bf16[1024,16,256]{2,1,0:T(8,128)(2,1)} %get-tuple-element.313, s32[2048]{0:T(1024)S(1)} %broadcast_clamp_fusion.2), kind=kCustom, calls=%fused_computation.clone.1 | custom fusion | bytes 33562624 | tf_op jit(solution)/shard_map/cond/branch_0_fun/while/body/eval_jaxpr/gather | solution.py:96
  458.1 11.7 %fusion.100 = (bf16[128,256,128]{2,1,0:T(8,128)(2,1)}, bf16[128,256,128]{2,1,0:T(8,128)(2,1)}) fusion(bf16[128,256,256]{2,1,0:T(8,128)(2,1)} %bitcast.134), kind=kLoop, calls=%fused_computation.121.clone.1 | loop fusion | bytes 33554432 | tf_op jit(solution)/shard_map/cond/branch_0_fun/while/body/eval_jaxpr/slice | solution.py:100
  470.6 7.1 %fusion.101 = (f32[128,8]{1,0:T(8,128)S(1)}, f32[128,8,257]{2,1,0:T(8,128)}) fusion(bf16[128,8,128]{2,1,0:T(8,128)(2,1)S(1)} %copy.103, bf16[128,1,128]{2,1,0:T(2,128)(2,1)S(1)} %copy.105, bf16[128,256,128]{2,1,0:T(8,128)(2,1)} %get-tuple-element.278, pred[128,257]{1,0:T(8,128)(4,1)S(1)} %concatenate.36), kind=kOutput, calls=%fused_computation.122.clone.1 | convolution fusion | flops 85266688 | bytes 9773184 | tf_op jit(solution)/shard_map/cond/branch_0_fun/while/body/eval_jaxpr/sub | solution.py:113
  484.8 121.6 %all-gather.4.cloned.1.call-done = bf16[512,8192]{0,1:T(8,128)(2,1)} async-done(((bf16[512,1024]{0,1:T(8,128)(2,1)}), bf16[512,8192]{0,1:T(8,128)(2,1)}) %all-gather.4.cloned.1.call-update) | async-done | bytes 8388624 | tf_op jit(solution)/shard_map/all_gather | solution.py:171
  606.4 15.6 %fusion.63 = bf16[1,512,1024]{2,1,0:T(8,128)(2,1)} fusion(bf16[512,8192]{0,1:T(8,128)(2,1)} %all-gather.4.cloned.1.call-done, bf16[8192,1024]{1,0:T(8,128)(2,1)} %get-tuple-element.209), kind=kOutput, calls=%fused_computation.79 | convolution fusion | flops 8590458880 | bytes 26214400 | tf_op jit(solution)/shard_map/dot_general | solution.py:170
  (140 shorter events, 60.3 us)
Async XLA Ops:
  6.5 245.7 %all-gather.6.cloned.1.call-start = ((), (), s32[]{:S(2)}) async-start(), calls=%async_computation.3 | async-start | bytes 9437184 | tf_op jit(solution)/shard_map/all_gather | solution.py:139
  13.7 12.6 %all-to-all-start.1 = ((bf16[8,8,1024]{2,0,1:T(8,128)(2,1)}), bf16[8,8,1024]{2,0,1:T(8,128)(2,1)S(1)}, u32[]{:S(2)}, u32[]{:S(2)}) async-start(bf16[8,8,1024]{2,0,1:T(8,128)(2,1)} %bitcast.31), calls=%async_computation.1 | async-start | bytes 262144 | tf_op jit(solution)/shard_map/all_to_all | solution.py:167
  20.1 11.4 %copy-start.7 = (s32[16]{0:T(128)S(1)}, s32[16]{0:T(128)}, u32[]{:S(2)}) copy-start(s32[16]{0:T(128)} %param.26) | copy-start | bytes 196
  20.1 11.9 %copy-start.3 = (bf16[64,1024]{1,0:T(8,128)(2,1)S(1)}, bf16[64,1024]{1,0:T(8,128)(2,1)}, u32[]{:S(2)}) copy-start(bf16[64,1024]{1,0:T(8,128)(2,1)} %param.20) | copy-start | bytes 393220
  20.1 11.9 %copy-start.6 = (bf16[8192]{0:T(1024)(128)(2,1)S(1)}, bf16[8192]{0:T(1024)(128)(2,1)}, u32[]{:S(2)}) copy-start(bf16[8192]{0:T(1024)(128)(2,1)} %param.18) | copy-start | bytes 49156
  20.1 12.2 %copy-start = (s32[32]{0:T(128)S(1)}, s32[32]{0:T(128)}, u32[]{:S(2)}) copy-start(s32[32]{0:T(128)} %param.27) | copy-start | bytes 388
  26.3 8.1 %copy-start.4 = (bf16[1,64,256]{2,1,0:T(8,128)(2,1)S(1)}, bf16[1,64,256]{2,1,0:T(8,128)(2,1)}, u32[]{:S(2)}) copy-start(bf16[1,64,256]{2,1,0:T(8,128)(2,1)} %param.22) | copy-start | bytes 98308
  26.3 8.1 %copy-start.2 = (s32[1,1024,256]{2,1,0:T(8,128)S(1)}, s32[1,1024,256]{2,1,0:T(8,128)}, u32[]{:S(2)}) copy-start(s32[1,1024,256]{2,1,0:T(8,128)} %param.21) | copy-start | bytes 3145732
  26.3 181.6 %all-to-all-start = ((s32[128,8,1024]{0,2,1:T(8,128)}), s32[128,8,1024]{0,2,1:T(8,128)}, u32[]{:S(2)}, u32[]{:S(2)}) async-start(s32[128,8,1024]{0,2,1:T(8,128)} %bitcast.139), calls=%async_computation | async-start | bytes 8388608 | tf_op jit(solution)/shard_map/all_to_all | solution.py:166
  31.4 6.3 copy-start.5
  31.4 6.4 %copy-start.8 = (s32[496]{0:T(512)S(1)}, s32[496]{0:T(512)}, u32[]{:S(2)}) copy-start(s32[496]{0:T(512)} %param.29) | copy-start | bytes 5956
  31.5 574.9 %all-gather.4.cloned.1.call-start = ((), (), s32[]{:S(2)}) async-start(), calls=%async_computation.2 | async-start | bytes 9437184 | tf_op jit(solution)/shard_map/all_gather | solution.py:171
  252.2 5.8 copy-start.1
  263.7 14.2 %collective-permute-start = (bf16[512,256]{0,1:T(8,128)(2,1)S(1)}, bf16[512,256]{0,1:T(8,128)(2,1)S(1)}, u32[]{:S(2)}, u32[]{:S(2)}) collective-permute-start(bf16[512,256]{0,1:T(8,128)(2,1)S(1)} %pad_maximum_fusion.1), channel_id=1, source_target_pairs={{0,1},{2,3},{4,5},{6,7},{8,9},{10,11},{12,13},{14,15},{16,17},{18,... | collective-permute-start | bytes 786440 | tf_op jit(solution)/shard_map/ppermute | solution.py:12
Sparse Core Ops, SparseCore 0:
  13.8 206.7 all-gather.5
  484.9 121.4 all-gather.3
where the time goes:
time: 632 us; the launch traced here: 629 us
  waiting for transfers between devices  291 us (46%)
  local copies, waits for them, and re-layouts  191 us (30%)
  matrix products  82.2 us (13%)
  other arithmetic  28.9 us (5%)
  between operations  13.7 us (2%)
  starting transfers between devices  13.1 us (2%)
  loops' own time  8.92 us (1%)
    all_to_all x1, waiting for transfers between devices, local(): lax.all_to_all(o_words, 'tp', split_axis=1, concat_axis=0, tiled=True)  169 us
    all_gather x1, waiting for transfers between devices, local(): lax.all_gather(attention_output, 'tp', axis=1, tiled=True)  122 us
    gather x4, local copies, waits for them, and re-layouts, decode_one_block(): pages = cache[part_table]  88.8 us
    slice x4, local copies, waits for them, and re-layouts, decode_one_block(): pages[..., :head_dim]  46.6 us
    sub x4, matrix products, decode_one_block(): attention_probs = jax.nn.softmax(logit_scores, axis=-1).astype(jnp.bfloat16)  28.2 us
    dot_general x1, local copies, waits for them, and re-layouts, local(): projected = jnp.dot(normed, w_query, preferred_element_type=jnp.float32)  21.3 us
    dot_general x4, matrix products, decode_one_block(): jnp.einsum('cwt,ctr->cwr', attention_probs, gathered_values, preferred_el...  21.1 us
    convert_element_type x2, other arithmetic, unpack_words(): return (values * spread).astype(jnp.bfloat16)  21 us
  transfers between devices with their start and end apart: 5, of which 3 were waited for; matrix products, arithmetic and copies ran while one was open for 11% of the time, Pallas kernels for 0%

commit v1 on v0

--- a/solution.py
+++ b/solution.py
@@ -1,6 +1,8 @@
 import jax
 import jax.numpy as jnp
 from jax import lax
+from jax.experimental import pallas as pl
+from jax.experimental.pallas import tpu as pltpu
 from jax.sharding import PartitionSpec as P
 
 HD = 128
@@ -83,41 +85,83 @@
     return done.reshape(rows, query.shape[1], query.shape[2])
 
 
-def decode_attend(query, key_self, value_self, cache, table, lengths):
-    rows = query.shape[0]
-    block = min(128, rows)
-    score_scale = query.shape[-1] ** (-0.5)
-    head_dim = query.shape[-1]
-
-    def decode_one_block(start):
-        partial_query = lax.dynamic_slice_in_dim(query, start, block, 0)
-        part_table = lax.dynamic_slice_in_dim(table, start, block, 0)
-        part_len = lax.dynamic_slice_in_dim(lengths, start, block, 0)
-        pages = cache[part_table]
-        pages = pages.reshape(block, pages.shape[1] * pages.shape[2], pages.shape[3])
-        own_key = lax.dynamic_slice_in_dim(key_self, start, block, 0)
-        own_value = lax.dynamic_slice_in_dim(value_self, start, block, 0)
-        gathered_keys = jnp.concatenate([pages[..., :head_dim], own_key[:, None, :]], axis=1)
-        gathered_values = jnp.concatenate([pages[..., head_dim:], own_value[:, None, :]], axis=1)
-        logit_scores = (
-            jnp.einsum(
-                "jai,jri->jar", partial_query, gathered_keys, preferred_element_type=jnp.float32
-            )
-            * score_scale
+def decode_kernel(table_ref, slots_ref, q_ref, own_ref, len_ref, fresh_ref, pool_ref, out_ref,
+                  cache, scores, weights, sem):
+    group, heads, head_dim = q_ref.shape
+    span = table_ref.shape[1]
+    page = cache.shape[1]
+    tokens = span * page
+    step = pl.program_id(0)
+
+    @pl.when(step == 0)
+    def _():
+        load = pltpu.make_async_copy(pool_ref, cache, sem)
+        load.start()
+        load.wait()
+
+        def place(j, carry):
+            cache[slots_ref[j]] = fresh_ref[j]
+            return carry
+
+        lax.fori_loop(0, slots_ref.shape[0], place, 0)
+
+    def pages(b, low):
+        picked = [
+            cache[table_ref[step * group + b, p], :, low : low + head_dim] for p in range(span)
+        ]
+        return jnp.concatenate(picked, axis=0)
+
+    for b in range(group):
+        scores[b] = lax.dot_general(
+            q_ref[b], pages(b, 0), (((1,), (1,)), ((), ())), preferred_element_type=jnp.float32
         )
-        spots = jnp.arange(pages.shape[1], dtype=jnp.int32)
-        valid = jnp.concatenate(
-            [spots[None, :] < part_len[:, None], jnp.ones((block, 1), dtype=bool)], axis=1
-        )
-        logit_scores = jnp.where(valid[:, None, :], logit_scores, -1e30)
-        attention_probs = jax.nn.softmax(logit_scores, axis=-1).astype(jnp.bfloat16)
-        return jnp.einsum(
-            "cwt,ctr->cwr", attention_probs, gathered_values, preferred_element_type=jnp.float32
+    scale = head_dim ** (-0.5)
+    spots = lax.broadcasted_iota(jnp.int32, (group, heads, tokens), 2)
+    valid = spots < len_ref[...][:, :, :1]
+    s = jnp.where(valid, scores[...] * scale, -1e30)
+    own_key = own_ref[:, :, :head_dim].astype(jnp.float32)
+    own_value = own_ref[:, :, head_dim:].astype(jnp.float32)
+    own = jnp.sum(q_ref[...].astype(jnp.float32) * own_key, axis=-1, keepdims=True) * scale
+    top = jnp.maximum(jnp.max(s, axis=-1, keepdims=True), own)
+    e = jnp.exp(s - top)
+    e_own = jnp.exp(own - top)
+    inverse = 1.0 / (jnp.sum(e, axis=-1, keepdims=True) + e_own)
+    weights[...] = (e * inverse).astype(jnp.bfloat16)
+    mine = (e_own * inverse).astype(jnp.bfloat16).astype(jnp.float32) * own_value
+    for b in range(group):
+        out_ref[b] = (
+            jnp.dot(weights[b], pages(b, head_dim), preferred_element_type=jnp.float32) + mine[b]
         ).astype(jnp.bfloat16)
 
-    starts = jnp.arange(0, rows, block, dtype=jnp.int32)
-    done = lax.map(decode_one_block, starts)
-    return done.reshape(rows, query.shape[1], query.shape[2])
+
+def decode_attend(query, own, fresh, pool, page_slots, table, lengths):
+    rows, heads, head_dim = query.shape
+    group = 16 if rows % 16 == 0 else 1
+    tokens = table.shape[1] * pool.shape[1]
+    wide = jnp.broadcast_to(lengths[:, None, None], (rows, 1, 128))
+    return pl.pallas_call(
+        decode_kernel,
+        grid_spec=pltpu.PrefetchScalarGridSpec(
+            num_scalar_prefetch=2,
+            grid=(rows // group,),
+            in_specs=[
+                pl.BlockSpec((group, heads, head_dim), lambda g, *_: (g, 0, 0)),
+                pl.BlockSpec((group, 1, 2 * head_dim), lambda g, *_: (g, 0, 0)),
+                pl.BlockSpec((group, 1, 128), lambda g, *_: (g, 0, 0)),
+                pl.BlockSpec(memory_space=pltpu.VMEM),
+                pl.BlockSpec(memory_space=pl.ANY),
+            ],
+            out_specs=pl.BlockSpec((group, heads, head_dim), lambda g, *_: (g, 0, 0)),
+            scratch_shapes=[
+                pltpu.VMEM(pool.shape, pool.dtype),
+                pltpu.VMEM((group, heads, tokens), jnp.float32),
+                pltpu.VMEM((group, heads, tokens), jnp.bfloat16),
+                pltpu.SemaphoreType.DMA(()),
+            ],
+        ),
+        out_shape=jax.ShapeDtypeStruct(query.shape, jnp.bfloat16),
+        compiler_params=pltpu.CompilerParams(vmem_limit_bytes=40 << 20),
+    )(table, page_slots, query, own[:, None, :], wide, fresh, pool)
 
 
 def local(
@@ -158,21 +202,16 @@
         return prefill_attend(query, key_new, value_new, doc)
 
     def run_decode():
-        cache = pool.at[page_slots].set(arrived.reshape(-1, pool.shape[1], pool.shape[2]))
-        return decode_attend(query, key_new, value_new, cache, table, lengths)
+        pages = arrived.reshape(-1, pool.shape[1], pool.shape[2])
+        return decode_attend(query, fresh, pages, pool, page_slots, table, lengths)
 
     attention_output = lax.cond(side == 0, run_prefill, run_decode).reshape(rows, -1)
-    column_words, column_scales = (
-        lax.all_to_all(o_words, "tp", split_axis=1, concat_axis=0, tiled=True),
-        lax.all_to_all(o_scales, "tp", split_axis=1, concat_axis=0, tiled=True),
-    )
-    w_columns = unpack_words(column_words, column_scales)
-    summed = jnp.dot(
-        lax.all_gather(attention_output, "tp", axis=1, tiled=True),
-        w_columns,
-        preferred_element_type=jnp.float32,
-    )
-    return summed.astype(jnp.bfloat16)[None]
+    w_rows = unpack_words(o_words, o_scales)
+    partial = jnp.dot(attention_output, w_rows, preferred_element_type=jnp.float32)
+    summed = lax.psum_scatter(
+        partial.astype(jnp.bfloat16), "tp", scatter_dimension=1, tiled=True
+    )
+    return summed[None]
 
 
 def solution(mesh):

time: 632 us -> 368 us (0.58)
  local copies, waits for them, and re-layouts: 191 us -> 33.9 us
  waiting for transfers between devices: 291 us -> 220 us
  matrix products: 82.2 us -> 31.4 us
  Pallas kernels: 0 us -> 32.9 us
  starting transfers between devices: 13.1 us -> 1.51 us
  loops' own time: 8.92 us -> 0.06 us
    all_to_all x2 -> x0, waiting for transfers between devices: 170 us -> none  [the longest x1 169 us: local(): lax.all_to_all(o_words, 'tp', split_axis=1, concat_axis=0, tiled=True)]
    reduce_scatter x0 -> x1, waiting for transfers between devices: none -> 146 us  [local(): lax.psum_scatter(partial.astype(jnp.bfloat16), 'tp', scatter_dimension=1,...]
    all_gather x1 -> x0, waiting for transfers between devices: 122 us -> none  [local(): lax.all_gather(attention_output, 'tp', axis=1, tiled=True)]
    gather x4 -> x0, local copies, waits for them, and re-layouts: 88.8 us -> none  [decode_one_block(): pages = cache[part_table]]
    all_gather x1, waiting for transfers between devices: 0.01 us -> 73.7 us  [local(): whole = lax.all_gather(rows_in[0], 'tp', axis=1, tiled=True)]
    slice x4 -> x0, local copies, waits for them, and re-layouts: 46.6 us -> none  [decode_one_block(): pages[..., :head_dim]]
    pallas_call x0 -> x1, Pallas kernels: none -> 32.9 us  [decode_attend(): pl.pallas_call(decode_kernel, grid_spec=pltpu.PrefetchScalarGridSpec(num_...]
    sub x4 -> x0, matrix products: 28.2 us -> none  [decode_one_block(): attention_probs = jax.nn.softmax(logit_scores, axis=-1).astype(jnp.bfloat16)]
  transfers between devices with their start and end apart: 5 -> 3, of which waited for: 3 -> 2; matrix products, arithmetic and copies ran while one was open for 11% -> 18% of each run, Pallas kernels for 0% -> 0%
where the time goes in v1:
time: 368 us; the launch traced here: 366 us
  waiting for transfers between devices  220 us (60%)
  local copies, waits for them, and re-layouts  33.9 us (9%)
  Pallas kernels  32.9 us (9%)
  other arithmetic  32.6 us (9%)
  matrix products  31.4 us (9%)
  between operations  13.7 us (4%)
    reduce_scatter x1, waiting for transfers between devices, local(): lax.psum_scatter(partial.astype(jnp.bfloat16), 'tp', scatter_dimension=1,...  146 us
    all_gather x1, waiting for transfers between devices, local(): whole = lax.all_gather(rows_in[0], 'tp', axis=1, tiled=True)  73.7 us
    pallas_call x1, Pallas kernels, decode_attend(): pl.pallas_call(decode_kernel, grid_spec=pltpu.PrefetchScalarGridSpec(num_...  32.9 us
    convert_element_type x3, other arithmetic, unpack_words(): return (values * spread).astype(jnp.bfloat16)  24.4 us
    dot_general x1, local copies, waits for them, and re-layouts, local(): projected = jnp.dot(normed, w_query, preferred_element_type=jnp.float32)  21.4 us
    dot_general x1, matrix products, local(): jnp.dot(attention_output, w_rows, preferred_element_type=jnp.float32)  14 us
    dot_general x1, matrix products, local(): projected = jnp.dot(normed, w_query, preferred_element_type=jnp.float32)  12.3 us
  transfers between devices with their start and end apart: 3, of which 2 were waited for; matrix products, arithmetic and copies ran while one was open for 18% of the time, Pallas kernels for 0%

profile of v1, /device:TPU:1, one launch (start us, length us, event | category | flops | bytes accessed | tf_op | source)
XLA Modules:
  0.0 366.4 jit_solution(17834144789160586216)
XLA Ops:
  6.5 0.7 all-gather.3.cloned.1.call-update
  7.4 0.7 copy.54
  8.3 0.7 and_select_fusion
  9.1 1.9 gather_fusion
  11.6 11.4 %fusion.26 = bf16[8192,1024]{1,0:T(8,128)(2,1)} fusion(f32[64,1024]{1,0:T(8,128)S(1)} %convert_element_type.83, s32[8192]{0:T(1024)S(1)} %shift_right_arithmetic.67, s32[1024,1024]{1,0:T(8,128)} %param.17), kind=kLoop, calls=%fused_computation.29 | loop fusion | flops 50331648 | bytes 21266432 | tf_op jit(solution)/shard_map/convert_element_type | solution.py:23
  23.0 21.4 %copy.72 = bf16[1024,8192]{1,0:T(8,128)(2,1)} copy(bf16[1024,8192]{0,1:T(8,128)(2,1)} %bitcast.108) | data formatting | bytes 33554432 | tf_op jit(solution)/shard_map/dot_general | solution.py:192
  44.4 3.3 fusion.35
  48.7 3.3 shift_right_arithmetic.74
  52.0 9.7 %fusion.25 = bf16[8,128,8192]{2,1,0:T(8,128)(2,1)} fusion(f32[8,8192]{1,0:T(8,128)S(1)} %convert_element_type.86, s32[128]{0:T(128)S(1)} %shift_right_arithmetic.77, s32[8,128,8192]{2,1,0:T(8,128)S(1)} %bitcast.107), kind=kLoop, calls=%fused_computation.27 | loop fusion | flops 50331648 | bytes 50594304 | tf_op jit(solution)/shard_map/convert_element_type | solution.py:23
  61.7 73.7 %all-gather.3.cloned.1.call-done = bf16[1,512,8192]{2,1,0:T(8,128)(2,1)} async-done(((bf16[1,512,1024]{2,1,0:T(8,128)(2,1)}), bf16[1,512,8192]{2,1,0:T(8,128)(2,1)}) %all-gather.3.cloned.1.call-update) | async-done | bytes 8388624 | tf_op jit(solution)/shard_map/all_gather | solution.py:183
  135.4 5.3 %fusion.30 = f32[512]{0:T(512)S(1)} fusion(bf16[1,512,8192]{2,1,0:T(8,128)(2,1)} %all-gather.3.cloned.1.call-done), kind=kLoop, calls=%fused_computation.36 | loop fusion | flops 12582400 | bytes 8390656 | tf_op jit(solution)/shard_map/reduce_sum | solution.py:28
  141.1 5.1 %fusion.40 = f32[512,256]{0,1:T(8,128)S(1)} fusion(bf16[8192,256]{1,0:T(8,128)(2,1)} %fusion.35, bf16[1,512,8192]{2,1,0:T(8,128)(2,1)S(1)} %copy-done.1, f32[8192]{0:T(1024)S(1)} %convert_element_type.74, f32[512]{0:T(512)S(1)} %add_rsqrt_fusion), kind=kOutput, calls=%fused_computation.48 | convolution fusion | flops 2164260864 | bytes 13142016 | tf_op jit(solution)/shard_map/dot_general | solution.py:194
  146.3 0.6 fusion.47
  146.9 1.5 collective-permute-start
  148.4 12.3 %fusion.33 = f32[512,8,128]{0,2,1:T(8,128)S(1)} fusion(bf16[8,128,8192]{2,1,0:T(8,128)(2,1)} %bitcast.109, bf16[1,512,8192]{2,1,0:T(8,128)(2,1)S(1)} %copy-done.1, f32[8192]{0:T(1024)S(1)} %convert_element_type.74, f32[512]{0:T(512)S(1)} %add_rsqrt_fusion), kind=kOutput, calls=%fused_computation.40 | convolution fusion | flops 8606711808 | bytes 27297792 | tf_op jit(solution)/shard_map/dot_general | solution.py:192
  161.2 0.6 broadcast_in_dim.100
  161.8 37.7 %conditional.1 = (bf16[512,8,128]{2,0,1:T(8,128)(2,1)S(1)}) conditional(s32[]{:T(128)} %convert_element_type.72, (bf16[512,256]{0,1:T(8,128)(2,1)S(1)}, s32[512]{0:T(512)S(1)}, bf16[512,256]{0,1:T(8,128)(2,1)S(1)}, bf16[1,1024,16,256]{3,2,1,0:T(8,128)(2,1)}, s32[512,16]{0,1:T(8,128)S(1)}, /*index=5*/s32[32]{0:T(128)S(1)}, ...), branch_computations={%region_3.4_spmd, %region_4.8_spmd} | conditional | flops 1087651840 | bytes 19738632 | solution.py:208
  161.8 0.7 copy-done.3
  162.5 0.7 copy.60.q_ref
  163.6 1.6 broadcast_in_dim.52.len_ref
  165.1 1.3 copy.51.own_ref
  166.4 32.9 %branch_0_fun.1 = bf16[512,8,128]{2,1,0:T(8,128)(2,1)S(1)} custom-call(s32[512,16]{1,0:T(8,128)S(1)} %copy.59.table_ref, s32[32]{0:T(128)S(1)} %get-tuple-element.60.slots_ref, bf16[512,8,128]{2,1,0:T(8,128)(2,1)S(1)} %copy.60.q_ref, bf16[512,1,256]{2,1,0:T(2,128)(2,1)S(1)} %copy.51.own_ref, s32[512,1,128]{2,1,0:T(1,128)S(1)} %broadcast_in_dim.52.len_ref, ...), custom_call_target="tpu_custom_call" | custom-call | tf_op jit(solution)/shard_map/cond/branch_0_fun/pallas_call | solution.py:142
  199.5 14.0 %bitcast_convert_fusion = bf16[512,8192]{1,0:T(8,128)(2,1)} fusion(bf16[512,8,128]{2,0,1:T(8,128)(2,1)S(1)} %get-tuple-element.134, bf16[8,128,8192]{2,1,0:T(8,128)(2,1)} %fusion.25), kind=kOutput, calls=%fused_computation.39 | convolution fusion | flops 8594128896 | bytes 26214400 | tf_op jit(solution)/shard_map/dot_general | solution.py:210
  213.5 146.1 %reduce-scatter.2.cloned.1.call-done = bf16[512,1024]{1,0:T(8,128)(2,1)} async-done(((bf16[512,8192]{1,0:T(8,128)(2,1)}), bf16[512,1024]{1,0:T(8,128)(2,1)}) %reduce-scatter.2.cloned.1.call-update) | async-done | bytes 1048592 | tf_op jit(solution)/shard_map/reduce_scatter | solution.py:211
  (59 shorter events, 3.3 us)
Async XLA Ops:
  6.5 4.7 %copy-start.10 = (bf16[8192]{0:T(1024)(128)(2,1)S(1)}, bf16[8192]{0:T(1024)(128)(2,1)}, u32[]{:S(2)}) copy-start(bf16[8192]{0:T(1024)(128)(2,1)} %param.16) | copy-start | bytes 49156
  6.5 4.7 %copy-start.6 = (bf16[64,1024]{1,0:T(8,128)(2,1)S(1)}, bf16[64,1024]{1,0:T(8,128)(2,1)}, u32[]{:S(2)}) copy-start(bf16[64,1024]{1,0:T(8,128)(2,1)} %param.18) | copy-start | bytes 393220
  6.5 4.7 %copy-start.7 = (bf16[8,8192]{1,0:T(8,128)(2,1)S(1)}, bf16[8,8192]{1,0:T(8,128)(2,1)}, u32[]{:S(2)}) copy-start(bf16[8,8192]{1,0:T(8,128)(2,1)} %param.22) | copy-start | bytes 393220
  6.5 128.8 %all-gather.3.cloned.1.call-start = ((), (), s32[]{:S(2)}) async-start(), calls=%async_computation.2 | async-start | bytes 9437184 | tf_op jit(solution)/shard_map/all_gather | solution.py:183
  7.3 352.3 %reduce-scatter.2.cloned.1.call-start = ((), (), s32[]{:S(2)}) async-start(), calls=%async_computation.1 | async-start | bytes 9437184 | tf_op jit(solution)/shard_map/reduce_scatter | solution.py:211
  23.0 21.5 %copy-start.8 = (bf16[1,64,256]{2,1,0:T(8,128)(2,1)S(1)}, bf16[1,64,256]{2,1,0:T(8,128)(2,1)}, u32[]{:S(2)}) copy-start(bf16[1,64,256]{2,1,0:T(8,128)(2,1)} %param.20) | copy-start | bytes 98308
  23.0 21.5 %copy-start.4 = (s32[1,1024,256]{2,1,0:T(8,128)S(1)}, s32[1,1024,256]{2,1,0:T(8,128)}, u32[]{:S(2)}) copy-start(s32[1,1024,256]{2,1,0:T(8,128)} %param.19) | copy-start | bytes 3145732
  23.0 24.8 %copy-start.9 = (s32[496,16]{0,1:T(8,128)S(1)}, s32[496,16]{0,1:T(8,128)}, u32[]{:S(2)}) copy-start(s32[496,16]{0,1:T(8,128)} %param.26) | copy-start | bytes 95236
  23.0 25.0 %copy-start.11 = (s32[496]{0:T(512)S(1)}, s32[496]{0:T(512)}, u32[]{:S(2)}) copy-start(s32[496]{0:T(512)} %param.27) | copy-start | bytes 5956
  44.4 4.3 %copy-start.2 = (s32[128,8192]{1,0:T(8,128)S(1)}, s32[128,8192]{1,0:T(8,128)}, u32[]{:S(2)}) copy-start(s32[128,8192]{1,0:T(8,128)} %param.21) | copy-start | bytes 12582916
  135.4 5.8 %copy-start.1 = (bf16[1,512,8192]{2,1,0:T(8,128)(2,1)S(1)}, bf16[1,512,8192]{2,1,0:T(8,128)(2,1)}, u32[]{:S(2)}) copy-start(bf16[1,512,8192]{2,1,0:T(8,128)(2,1)} %all-gather.3.cloned.1.call-done) | copy-start | bytes 25165828
  146.8 1.5 copy-start.5
  146.9 14.9 %collective-permute-start = (bf16[512,256]{0,1:T(8,128)(2,1)S(1)}, bf16[512,256]{0,1:T(8,128)(2,1)S(1)}, u32[]{:S(2)}, u32[]{:S(2)}) collective-permute-start(bf16[512,256]{0,1:T(8,128)(2,1)S(1)} %pad_maximum_fusion.1), channel_id=1, source_target_pairs={{0,1},{2,3},{4,5},{6,7},{8,9},{10,11},{12,13},{14,15},{16,17},{18,... | collective-permute-start | bytes 786440 | tf_op jit(solution)/shard_map/ppermute | solution.py:14
  148.4 13.5 %copy-start = (s32[32]{0:T(128)S(1)}, s32[32]{0:T(128)}, u32[]{:S(2)}) copy-start(s32[32]{0:T(128)} %param.25) | copy-start | bytes 388
  161.8 0.7 copy-start.3
Sparse Core Ops, SparseCore 0:
  9.5 125.7 all-gather.2
  213.6 145.9 reduce-scatter.1

commit v2 on v1

--- a/solution.py
+++ b/solution.py
@@ -1,3 +1,5 @@
+import functools
+
 import jax
 import jax.numpy as jnp
 from jax import lax
@@ -162,6 +164,205 @@
         out_shape=jax.ShapeDtypeStruct(query.shape, jnp.bfloat16),
         compiler_params=pltpu.CompilerParams(vmem_limit_bytes=40 << 20),
     )(table, page_slots, query, own[:, None, :], wide, fresh, pool)
+
+
+def project_kernel(n, pair, x_ref, w_ref, out_ref, w_here, y_out, y_in, z_out, up_in, down_in,
+                   w_sem, y_sent, y_got, z_sent, up_got, down_got):
+    me = lax.axis_index("tp")
+    length = n // pair
+    z, y = me // pair, me % pair
+    width = out_ref.shape[1]
+    tile = min(256, width)
+    tiles = width // tile
+
+    def greet(device):
+        pl.semaphore_signal(
+            barrier, inc=1, device_id={"tp": device}, device_id_type=pl.DeviceIdType.MESH
+        )
+
+    def load(dest):
+        start = pl.multiple_of(dest * width, width)
+        return pltpu.make_async_copy(
+            w_ref.at[:, pl.ds(start, width)], w_here.at[dest], w_sem.at[dest]
+        )
+
+    def send(source, target, sent, got, device):
+        return pltpu.make_async_remote_copy(
+            src_ref=source,
+            dst_ref=target,
+            send_sem=sent,
+            recv_sem=got,
+            device_id={"tp": device},
+            device_id_type=pl.DeviceIdType.MESH,
+        )
+
+    def across(d):
+        return send(y_out.at[d], y_in.at[d], y_sent.at[d], y_got.at[d], z * pair + 1 - y)
+
+    def upward(d):
+        return send(z_out.at[d], up_in.at[d], z_sent.at[d], up_got.at[d], me + pair)
+
+    def downward(d):
+        return send(z_out.at[d], down_in.at[d], z_sent.at[d], down_got.at[d], me - pair)
+
+    def in_order(above, below):
+        def both(j, carry):
+            @pl.when(length - 1 - j > z)
+            def _():
+                above(length - 1 - j)
+
+            @pl.when(j < z)
+            def _():
+                below(j)
+
+            return carry
+
+        lax.fori_loop(0, length - 1, both, 0)
+
+    def product(dest, put):
+        load(dest).wait()
+
+        def one(c, carry):
+            columns = pl.ds(pl.multiple_of(c * tile, tile), tile)
+            put(
+                columns,
+                jnp.dot(x_ref[...], w_here[dest, :, columns], preferred_element_type=jnp.float32),
+            )
+            return carry
+
+        lax.fori_loop(0, tiles, one, 0)
+
+    def swap(d):
+        def put(columns, value):
+            y_out[d, :, columns] = value.astype(jnp.bfloat16)
+
+        product(d * pair + 1 - y, put)
+        across(d).start()
+
+    def total(d, target, extra):
+        if pair > 1:
+            across(d).wait_recv()
+
+        def put(columns, value):
+            if pair > 1:
+                value = value + y_in[d, :, columns].astype(jnp.float32)
+            for block in extra:
+                value = value + block[d, :, columns].astype(jnp.float32)
+            target(columns, value.astype(jnp.bfloat16))
+
+        product(d * pair + y, put)
+
+    def chain(d, arriving, got, has, pass_on):
+        def store(columns, value):
+            z_out[d, :, columns] = value
+
+        @pl.when(has)
+        def _():
+            got(d).wait_recv()
+            total(d, store, (arriving,))
+
+        @pl.when(jnp.logical_not(has))
+        def _():
+            total(d, store, ())
+
+        pass_on(d).start()
+
+    if pair > 1:
+        in_order(
+            lambda d: load(d * pair + 1 - y).start(), lambda d: load(d * pair + 1 - y).start()
+        )
+        load(z * pair + 1 - y).start()
+    in_order(lambda d: load(d * pair + y).start(), lambda d: load(d * pair + y).start())
+    load(z * pair + y).start()
+
+    barrier = pltpu.get_barrier_semaphore()
+    has_lower, has_upper = z > 0, z < length - 1
+    if pair > 1:
+        greet(z * pair + 1 - y)
+
+    @pl.when(has_lower)
+    def _():
+        greet(me - pair)
+
+    @pl.when(has_upper)
+    def _():
+        greet(me + pair)
+
+    lower, upper = (z + length - 1) // length, 1 - (z + 1) // length
+    pl.semaphore_wait(barrier, pair - 1 + lower + upper)
+
+    if pair > 1:
+        in_order(swap, swap)
+        swap(z)
+    in_order(
+        lambda d: chain(d, up_in, upward, has_lower, upward),
+        lambda d: chain(d, down_in, downward, has_upper, downward),
+    )
+
+    def finish(columns, value):
+        out_ref[:, columns] = value
+
+    @pl.when(has_lower)
+    def _():
+        upward(z).wait_recv()
+
+    @pl.when(has_upper)
+    def _():
+        downward(z).wait_recv()
+
+    @pl.when(jnp.logical_and(has_lower, has_upper))
+    def _():
+        total(z, finish, (up_in, down_in))
+
+    @pl.when(jnp.logical_and(has_lower, jnp.logical_not(has_upper)))
+    def _():
+        total(z, finish, (up_in,))
+
+    @pl.when(jnp.logical_and(has_upper, jnp.logical_not(has_lower)))
+    def _():
+        total(z, finish, (down_in,))
+
+    in_order(lambda d: upward(d).wait_send(), lambda d: downward(d).wait_send())
+    if pair > 1:
+        in_order(lambda d: across(d).wait_send(), lambda d: across(d).wait_send())
+        across(z).wait_send()
+
+
+def project(x, w):
+    n = lax.axis_size("tp")
+    pair = 2 if n == 8 else 1
+    length = n // pair
+    rows, depth = x.shape
+    width = w.shape[1] // n
+    slots = pltpu.VMEM((length, rows, width), jnp.bfloat16)
+    crossing = slots if pair > 1 else pltpu.VMEM((1, 16, 128), jnp.bfloat16)
+    dma = pltpu.SemaphoreType.DMA((length,))
+    return pl.pallas_call(
+        functools.partial(project_kernel, n, pair),
+        out_shape=jax.ShapeDtypeStruct((rows, width), jnp.bfloat16),
+        in_specs=[
+            pl.BlockSpec(memory_space=pltpu.VMEM),
+            pl.BlockSpec(memory_space=pl.ANY),
+        ],
+        out_specs=pl.BlockSpec(memory_space=pltpu.VMEM),
+        scratch_shapes=[
+            pltpu.VMEM((n, depth, width), jnp.bfloat16),
+            crossing,
+            crossing,
+            slots,
+            slots,
+            slots,
+            pltpu.SemaphoreType.DMA((n,)),
+            dma,
+            dma,
+            dma,
+            dma,
+            dma,
+        ],
+        compiler_params=pltpu.CompilerParams(
+            collective_id=0, has_side_effects=True, vmem_limit_bytes=58 << 20
+        ),
+    )(x, w)
 
 
 def local(
@@ -207,10 +408,7 @@
 
     attention_output = lax.cond(side == 0, run_prefill, run_decode).reshape(rows, -1)
     w_rows = unpack_words(o_words, o_scales)
-    partial = jnp.dot(attention_output, w_rows, preferred_element_type=jnp.float32)
-    summed = lax.psum_scatter(
-        partial.astype(jnp.bfloat16), "tp", scatter_dimension=1, tiled=True
-    )
+    summed = project(attention_output, w_rows)
     return summed[None]
 
 

time: 368 us -> 312 us (0.85)
  waiting for transfers between devices: 220 us -> 77.8 us
  Pallas kernels: 32.9 us -> 136 us
  matrix products: 31.4 us -> 17.4 us
    reduce_scatter x1 -> x0, waiting for transfers between devices: 146 us -> none  [local(): lax.psum_scatter(partial.astype(jnp.bfloat16), 'tp', scatter_dimension=1,...]
    pallas_call x0 -> x1, Pallas kernels: none -> 103 us  [project(): pl.pallas_call(functools.partial(project_kernel, n, pair), out_shape=jax....]
    dot_general x1 -> x0, matrix products: 14 us -> none  [local(): jnp.dot(attention_output, w_rows, preferred_element_type=jnp.float32)]
  transfers between devices with their start and end apart: 3 -> 2, of which waited for: 2 -> 1; matrix products, arithmetic and copies ran while one was open for 18% -> 21% of each run, Pallas kernels for 0% -> 0%
where the time goes in v2:
time: 312 us; the launch traced here: 311 us
  Pallas kernels  136 us (44%)
  waiting for transfers between devices  77.8 us (25%)
  other arithmetic  32.5 us (10%)
  local copies, waits for them, and re-layouts  32.4 us (10%)
  matrix products  17.4 us (6%)
  between operations  13.6 us (4%)
    pallas_call x1, Pallas kernels, project(): pl.pallas_call(functools.partial(project_kernel, n, pair), out_shape=jax....  103 us
    all_gather x1, waiting for transfers between devices, local(): whole = lax.all_gather(rows_in[0], 'tp', axis=1, tiled=True)  77.1 us
    pallas_call x1, Pallas kernels, decode_attend(): pl.pallas_call(decode_kernel, grid_spec=pltpu.PrefetchScalarGridSpec(num_...  32.9 us
    convert_element_type x3, other arithmetic, unpack_words(): return (values * spread).astype(jnp.bfloat16)  24.1 us
    dot_general x1, local copies, waits for them, and re-layouts, local(): projected = jnp.dot(normed, w_query, preferred_element_type=jnp.float32)  21.5 us
    dot_general x1, matrix products, local(): projected = jnp.dot(normed, w_query, preferred_element_type=jnp.float32)  12.3 us
  transfers between devices with their start and end apart: 2, of which 1 were waited for; matrix products, arithmetic and copies ran while one was open for 21% of the time, Pallas kernels for 0%

profile of v2, /device:TPU:1, one launch (start us, length us, event | category | flops | bytes accessed | tf_op | source)
XLA Modules:
  0.0 311.1 jit_solution(13755180797254199108)
XLA Ops:
  6.5 0.7 all-gather.3.cloned.1.call-update
  7.3 0.7 copy.54
  8.3 0.9 convert_element_type.78
  9.3 11.3 %fusion.24 = bf16[8192,1024]{1,0:T(8,128)(2,1)} fusion(f32[64,1024]{1,0:T(8,128)S(1)} %convert_element_type.78, s32[8192]{0:T(1024)S(1)} %shift_right_arithmetic.66, s32[1024,1024]{1,0:T(8,128)} %param.17), kind=kLoop, calls=%fused_computation.28 | loop fusion | flops 50331648 | bytes 21266432 | tf_op jit(solution)/shard_map/convert_element_type | solution.py:25
  20.6 21.5 %copy.71 = bf16[1024,8192]{1,0:T(8,128)(2,1)} copy(bf16[1024,8192]{0,1:T(8,128)(2,1)} %bitcast.106) | data formatting | bytes 33554432 | tf_op jit(solution)/shard_map/dot_general | solution.py:393
  42.4 1.9 gather_fusion
  44.6 3.3 %fusion.33 = bf16[8192,256]{1,0:T(8,128)(2,1)} fusion(f32[64,256]{1,0:T(8,128)S(1)} %bitcast_convert_fusion, s32[8192]{0:T(1024)S(1)} %shift_right_arithmetic.66, s32[1024,256]{1,0:T(8,128)S(1)} %bitcast.113), kind=kLoop, calls=%fused_computation.41 | loop fusion | flops 12582912 | bytes 5341184 | tf_op jit(solution)/shard_map/convert_element_type | solution.py:25
  48.0 9.4 %fusion.20.w_ref = bf16[1024,8192]{1,0:T(8,128)(2,1)} fusion(f32[8,8192]{1,0:T(8,128)S(1)} %convert_element_type.81, s32[1024]{0:T(1024)S(1)} %shift_right_arithmetic.76, s32[128,8192]{1,0:T(8,128)S(1)} %copy-done.2), kind=kLoop, calls=%fused_computation.22 | loop fusion | flops 50331648 | bytes 21237760 | tf_op jit(solution)/shard_map/convert_element_type | solution.py:25
  57.8 0.5 multiply_cosine_fusion
  58.3 77.1 %all-gather.3.cloned.1.call-done = bf16[1,512,8192]{2,1,0:T(8,128)(2,1)} async-done(((bf16[1,512,1024]{2,1,0:T(8,128)(2,1)}), bf16[1,512,8192]{2,1,0:T(8,128)(2,1)}) %all-gather.3.cloned.1.call-update) | async-done | bytes 8388624 | tf_op jit(solution)/shard_map/all_gather | solution.py:384
  135.4 5.3 %fusion.28 = f32[512]{0:T(512)S(1)} fusion(bf16[1,512,8192]{2,1,0:T(8,128)(2,1)} %all-gather.3.cloned.1.call-done), kind=kLoop, calls=%fused_computation.35 | loop fusion | flops 12582400 | bytes 8390656 | tf_op jit(solution)/shard_map/reduce_sum | solution.py:30
  141.1 5.1 %fusion.38 = f32[512,256]{0,1:T(8,128)S(1)} fusion(bf16[8192,256]{1,0:T(8,128)(2,1)} %fusion.33, bf16[1,512,8192]{2,1,0:T(8,128)(2,1)S(1)} %copy-done.1, f32[8192]{0:T(1024)S(1)} %convert_element_type.69, f32[512]{0:T(512)S(1)} %add_rsqrt_fusion), kind=kOutput, calls=%fused_computation.46 | convolution fusion | flops 2164260864 | bytes 13142016 | tf_op jit(solution)/shard_map/dot_general | solution.py:395
  146.3 0.6 fusion.45
  146.9 1.5 collective-permute-start
  148.4 12.3 %fusion.31 = f32[512,8,128]{0,2,1:T(8,128)S(1)} fusion(bf16[8,128,8192]{2,1,0:T(8,128)(2,1)} %bitcast.107, bf16[1,512,8192]{2,1,0:T(8,128)(2,1)S(1)} %copy-done.1, f32[8192]{0:T(1024)S(1)} %convert_element_type.69, f32[512]{0:T(512)S(1)} %add_rsqrt_fusion), kind=kOutput, calls=%fused_computation.38 | convolution fusion | flops 8606711808 | bytes 27297792 | tf_op jit(solution)/shard_map/dot_general | solution.py:393
  161.2 0.6 broadcast_in_dim.100
  161.8 37.2 %conditional.1 = (bf16[512,1024]{1,0:T(8,128)(2,1)S(1)}) conditional(s32[]{:T(128)} %convert_element_type.67, (bf16[512,256]{0,1:T(8,128)(2,1)S(1)}, s32[512]{0:T(512)S(1)}, bf16[512,256]{0,1:T(8,128)(2,1)S(1)}, bf16[1,1024,16,256]{3,2,1,0:T(8,128)(2,1)}, s32[512,16]{0,1:T(8,128)S(1)}, /*index=5*/s32[32]{0:T(128)S(1)}, ...), branch_computations={%region_3.4_spmd, %region_4.8_spmd} | conditional | flops 1087651840 | bytes 21835784 | solution.py:409
  161.8 0.7 copy.60.q_ref
  163.1 1.6 broadcast_in_dim.52.len_ref
  164.8 32.9 %branch_0_fun.1 = bf16[512,8,128]{2,1,0:T(8,128)(2,1)S(1)} custom-call(s32[512,16]{1,0:T(8,128)S(1)} %copy.59.table_ref, s32[32]{0:T(128)S(1)} %get-tuple-element.61.slots_ref, bf16[512,8,128]{2,1,0:T(8,128)(2,1)S(1)} %copy.60.q_ref, bf16[512,1,256]{2,1,0:T(2,128)(2,1)S(1)} %copy.51.own_ref, s32[512,1,128]{2,1,0:T(1,128)S(1)} %broadcast_in_dim.52.len_ref, ...), custom_call_target="tpu_custom_call" | custom-call | tf_op jit(solution)/shard_map/cond/branch_0_fun/pallas_call | solution.py:144
  197.8 0.7 copy.69
  198.5 0.5 copy.72
  199.0 102.9 %shard_map.128 = bf16[512,1024]{1,0:T(8,128)(2,1)} custom-call(bf16[512,1024]{1,0:T(8,128)(2,1)S(1)} %get-tuple-element.122.x_ref, bf16[1024,8192]{1,0:T(8,128)(2,1)} %fusion.20.w_ref), custom_call_target="tpu_custom_call" | custom-call | tf_op jit(solution)/shard_map/pallas_call | solution.py:340
  302.0 2.3 copy.77
  (53 shorter events, 3.0 us)
Async XLA Ops:
  6.5 128.8 %all-gather.3.cloned.1.call-start = ((), (), s32[]{:S(2)}) async-start(), calls=%async_computation | async-start | bytes 9437184 | tf_op jit(solution)/shard_map/all_gather | solution.py:384
  20.6 21.5 %copy-start.7 = (bf16[8192]{0:T(1024)(128)(2,1)S(1)}, bf16[8192]{0:T(1024)(128)(2,1)}, u32[]{:S(2)}) copy-start(bf16[8192]{0:T(1024)(128)(2,1)} %param.16) | copy-start | bytes 49156
  20.6 21.6 %copy-start.8 = (s32[16]{0:T(128)S(1)}, s32[16]{0:T(128)}, u32[]{:S(2)}) copy-start(s32[16]{0:T(128)} %param.24) | copy-start | bytes 196
  20.6 21.8 %copy-start = (s32[32]{0:T(128)S(1)}, s32[32]{0:T(128)}, u32[]{:S(2)}) copy-start(s32[32]{0:T(128)} %param.25) | copy-start | bytes 388
  42.1 2.5 copy-start.4
  42.1 2.5 copy-start.5
  42.1 2.5 copy-start.3
  44.6 3.4 %copy-start.2 = (s32[128,8192]{1,0:T(8,128)S(1)}, s32[128,8192]{1,0:T(8,128)}, u32[]{:S(2)}) copy-start(s32[128,8192]{1,0:T(8,128)} %param.21) | copy-start | bytes 12582916
  48.0 9.5 %copy-start.6 = (s32[496,16]{0,1:T(8,128)S(1)}, s32[496,16]{0,1:T(8,128)}, u32[]{:S(2)}) copy-start(s32[496,16]{0,1:T(8,128)} %param.26) | copy-start | bytes 95236
  48.0 9.6 %copy-start.9 = (s32[496]{0:T(512)S(1)}, s32[496]{0:T(512)}, u32[]{:S(2)}) copy-start(s32[496]{0:T(512)} %param.27) | copy-start | bytes 5956
  135.4 5.8 %copy-start.1 = (bf16[1,512,8192]{2,1,0:T(8,128)(2,1)S(1)}, bf16[1,512,8192]{2,1,0:T(8,128)(2,1)}, u32[]{:S(2)}) copy-start(bf16[1,512,8192]{2,1,0:T(8,128)(2,1)} %all-gather.3.cloned.1.call-done) | copy-start | bytes 25165828
  146.9 14.9 %collective-permute-start = (bf16[512,256]{0,1:T(8,128)(2,1)S(1)}, bf16[512,256]{0,1:T(8,128)(2,1)S(1)}, u32[]{:S(2)}, u32[]{:S(2)}) collective-permute-start(bf16[512,256]{0,1:T(8,128)(2,1)S(1)} %pad_maximum_fusion.1), channel_id=1, source_target_pairs={{0,1},{2,3},{4,5},{6,7},{8,9},{10,11},{12,13},{14,15},{16,17},{18,... | collective-permute-start | bytes 786440 | tf_op jit(solution)/shard_map/ppermute | solution.py:16
Sparse Core Ops, SparseCore 0:
  9.5 125.7 all-gather.2
